TPU v7x, 32 devices: a whole 2x2x4 slice. The times are simulated.
32 devices in a mesh: groups: 2 (over y), tensor: 4 (over z), section: 2 (over x), split: 2 (over core).
Axes of the slice: x: 2, y: 2, z: 4, core: 2. Of those that a mesh axis runs over, the one named last changes fastest.
Arguments:
- teacher_hidden: bfloat16 [1024, 16384], P(('groups', 'section', 'split'), 'tensor'), parts along dimension 0, may hold values from -60 to 60, as said below
- teacher_gain: float32 [16384], P('tensor'), may hold values from 0.1 to 1.9
- proj_weight: bfloat16 [16384, 4096], P(('tensor', 'section'), 'split'), may hold values from -0.046875 to 0.046875
- student_input: bfloat16 [1024, 4096], P(('groups', 'split'), ('tensor', 'section')), parts along dimension 0, may hold values from -6 to 6
- student_gain: bfloat16 [4096], P(('tensor', 'section')), may hold values from 0.099609375 to 1.8984375
- gate_weight: bfloat16 [4096, 14336], P(None, ('tensor', 'section')), may hold values from -0.09375 to 0.09375
- up_weight: bfloat16 [4096, 14336], P(None, ('tensor', 'section')), may hold values from -0.09375 to 0.09375
- down_weight: bfloat16 [14336, 4096], P(('tensor', 'section')), may hold values from -0.046875 to 0.046875
- block_order: int32 [256], replicated, may hold values from 0 to 255, each once
Outputs:
- grad_gate: bfloat16 [8192, 14336], P(('groups', 'split'), ('tensor', 'section')), parts along dimension 0
- grad_up: bfloat16 [8192, 14336], P(('groups', 'split'), ('tensor', 'section')), parts along dimension 0
- grad_down: bfloat16 [28672, 4096], P(('groups', 'tensor', 'section'), 'split'), parts along dimension 0
There are 2 independent parts, one for each index of `groups`. A program takes and returns all parts, laid end to end along the dimension named above; an argument that names none is the same for every part. Nothing has to cross between parts.
Inputs may be any that keep to these rules, and one draw needn't show every extreme that they name: `teacher_hidden`: teacher hidden states; rows differ in scale.
All inputs are finite; a program needn't handle non-finite values.
Results may differ from a plain program's by a relative error of at most 0.0083.
Values may be sent and summed in bfloat16 or wider, within the bound.
A program may use at most 256 MiB of HBM per device.

v0:
```python
import jax
import jax.numpy as jnp
from jax import lax
from jax.sharding import PartitionSpec as P


def swapped(value, axis, bit):
    mask = 2**bit
    pairs = [(source, source ^ mask) for source in range(lax.axis_size(axis))]
    return lax.ppermute(value, axis, pairs)


def on_device(
    teacher_hidden,
    teacher_gain,
    proj_weight,
    student_input,
    student_gain,
    gate_weight,
    up_weight,
    down_weight,
    block_order,
):
    eps = 1e-05
    whole_input, whole_gain = (
        lax.all_gather(student_input, ("tensor", "section"), axis=1, tiled=True),
        lax.all_gather(student_gain, ("tensor", "section"), axis=0, tiled=True),
    )
    shard_rows = whole_input.shape[0]
    inputs = whole_input.astype(jnp.float32)
    stu_sq = jnp.mean(inputs * inputs, axis=1, keepdims=True)
    normed = (inputs * lax.rsqrt(stu_sq + eps) * whole_gain.astype(jnp.float32)).astype(
        jnp.bfloat16
    )
    gate = jnp.dot(normed, gate_weight, preferred_element_type=jnp.float32)
    up = jnp.dot(normed, up_weight, preferred_element_type=jnp.float32)
    active = jax.nn.silu(gate)
    hidden = (active * up).astype(jnp.bfloat16)
    output_part = jnp.dot(hidden, down_weight, preferred_element_type=jnp.float32)
    sections = lax.axis_size("section")
    moved = lax.all_to_all(teacher_hidden, "section", split_axis=1, concat_axis=0, tiled=True)
    teach = moved.astype(jnp.float32)
    local_sq = jnp.sum(teach * teach, axis=1)
    total_sq = lax.psum(local_sq, ("tensor", "section"))
    narrow = moved.shape[1]
    width = narrow * lax.axis_size("tensor") * sections
    piece_gain = lax.dynamic_slice_in_dim(
        teacher_gain, lax.axis_index("section") * narrow, narrow, 0
    )
    scaled = teach * lax.rsqrt(total_sq / width + eps)[:, None] * piece_gain
    teacher_normed = scaled.astype(jnp.bfloat16)
    arranged = jnp.take(teacher_normed, block_order, axis=0)
    target_part = jnp.dot(
        arranged,
        lax.all_gather(proj_weight, "split", axis=1, tiled=True),
        preferred_element_type=jnp.float32,
    )
    output_part = output_part - target_part
    total_rows = shard_rows * lax.axis_size("split")
    difference = inputs + lax.psum(output_part, ("tensor", "section"))
    cotangent = (difference * (64.0 / total_rows)).astype(jnp.bfloat16)
    back_hidden = lax.dot_general(
        cotangent, down_weight, (((1,), (1,)), ((), ())), preferred_element_type=jnp.float32
    )
    sigma = jax.nn.sigmoid(gate)
    d_gate = (back_hidden * up * sigma * (1.0 + gate * (1.0 - sigma))).astype(jnp.bfloat16)
    d_up = (back_hidden * active).astype(jnp.bfloat16)
    contract_rows = (((0,), (0,)), ((), ()))
    part_gate = lax.dot_general(
        normed, d_gate, contract_rows, preferred_element_type=jnp.float32
    ).astype(jnp.bfloat16)
    part_up = lax.dot_general(
        normed, d_up, contract_rows, preferred_element_type=jnp.float32
    ).astype(jnp.bfloat16)
    part_down = lax.dot_general(
        hidden, cotangent, contract_rows, preferred_element_type=jnp.float32
    ).astype(jnp.bfloat16)
    mine_index = lax.axis_index("split")
    other_index = 1 - mine_index
    half_rows = part_gate.shape[0] // 2
    half_cols = part_down.shape[1] // 2
    keep_gate = lax.dynamic_slice_in_dim(part_gate, mine_index * half_rows, half_rows, 0)
    keep_up = lax.dynamic_slice_in_dim(part_up, mine_index * half_rows, half_rows, 0)
    keep_down = lax.dynamic_slice_in_dim(part_down, mine_index * half_cols, half_cols, 1)
    send_gate = lax.dynamic_slice_in_dim(part_gate, other_index * half_rows, half_rows, 0)
    send_up = lax.dynamic_slice_in_dim(part_up, other_index * half_rows, half_rows, 0)
    send_down = lax.dynamic_slice_in_dim(part_down, other_index * half_cols, half_cols, 1)
    got_gate, got_up, got_down = swapped((send_gate, send_up, send_down), "split", 0)
    summed_gate = keep_gate.astype(jnp.float32) + got_gate.astype(jnp.float32)
    summed_up = keep_up.astype(jnp.float32) + got_up.astype(jnp.float32)
    summed_down = keep_down.astype(jnp.float32) + got_down.astype(jnp.float32)
    return (
        summed_gate.astype(jnp.bfloat16),
        summed_up.astype(jnp.bfloat16),
        summed_down.astype(jnp.bfloat16),
    )


def solution(mesh):
    placed = (
        P(("groups", "section", "split"), "tensor"),
        P("tensor"),
        P(("tensor", "section"), "split"),
        P(("groups", "split"), ("tensor", "section")),
        P(("tensor", "section")),
        P(None, ("tensor", "section")),
        P(None, ("tensor", "section")),
        P(("tensor", "section"), None),
        P(),
    )
    return jax.shard_map(
        on_device,
        mesh=mesh,
        in_specs=placed,
        out_specs=(
            P(("groups", "split"), ("tensor", "section")),
            P(("groups", "split"), ("tensor", "section")),
            P(("groups", "tensor", "section"), "split"),
        ),
        check_vma=False,
    )
```

profile of v0, /device:TPU:1, one launch (start us, length us, event | category | flops | bytes accessed | tf_op | source)
XLA Modules:
  0.0 381.0 jit_solution(15152893474463836444)
XLA Ops:
  7.2 0.7 all-gather.4.cloned.1.call-update
  8.0 0.7 all-gather.6.cloned.1.call-update
  8.7 0.4 copy-done.1
  9.1 1.0 copy.17
  10.2 3.6 all-to-all-start
  13.8 0.0 all-reduce.2.cloned.1.call-start
  13.8 34.1 %all-gather = bf16[8,1,512]{2,1,0:T(2,128)(2,1)S(1)} all-gather(bf16[1,1,512]{2,1,0:T(2,128)(2,1)S(1)} %reshape.38), channel_id=1, replica_groups=mesh['groups'=2,'tensor'=4,'section'=2,'split'=2] {'tensor','section'}, dimensions={0}, use_global_device_ids=true | all-gather | bytes 9216 | tf_op jit(solution)/shard_map/all_gather | solution.py:27
  48.1 0.3 multiply_reduce_fusion
  48.4 16.4 %psum.14 = f32[256]{0:T(256)S(1)} all-reduce(f32[256]{0:T(256)S(1)} %bitcast.28), channel_id=1, replica_groups=mesh['groups'=2,'tensor'=4,'section'=2,'split'=2] {'tensor','section'}, use_global_device_ids=true, to_apply=%region_2.3 | all-reduce | flops 256 | bytes 2048 | tf_op jit(solution)/shard_map/psum | solution.py:44
  64.7 0.3 fusion.6
  65.0 2.3 gather_fusion
  67.4 2.2 fusion
  69.7 12.1 %fusion.23 = f32[256,1792]{1,0:T(8,128)S(1)} fusion(bf16[4096,1792]{1,0:T(8,128)(2,1)} %param.14, bf16[256,4096]{1,0:T(8,128)(2,1)} %all-gather.4.cloned.1.call-done, f32[4096]{0:T(1024)S(1)} %bitcast.24, f32[256]{0:T(256)S(1)} %add_rsqrt_fusion.1), kind=kOutput, calls=%fused_computation.43 | convolution fusion | flops 3762290688 | bytes 18629632 | tf_op jit(solution)/shard_map/dot_general | solution.py:35
  81.8 0.3 slice-done.1
  82.1 2.1 slice-done.2
  84.2 0.9 slice-done.3
  85.1 5.3 %multiply_convert_fusion.2 = (bf16[256,1792]{1,0:T(8,128)(2,1)S(1)}, f32[256,1792]{1,0:T(8,128)}) fusion(f32[256,1792]{1,0:T(8,128)S(1)} %fusion.23, bf16[4096,1792]{1,0:T(8,128)(2,1)S(1)} %bitcast.30, bf16[256,4096]{1,0:T(8,128)(2,1)S(1)} %copy-done, f32[4096]{0:T(1024)S(1)} %bitcast.25, f32[256]{0:T(256)S(1)} %add_rsqrt_fusion.1), kind=kOutput, calls=%fused_computation.22 | convolution fusion | flops 3765043200 | bytes 21382144 | tf_op jit(solution)/shard_map/dot_general | solution.py:36
  90.4 10.6 %fusion.25 = f32[256,4096]{1,0:T(8,128)} fusion(bf16[256,1792]{1,0:T(8,128)(2,1)S(1)} %get-tuple-element.3, bf16[1792,4096]{1,0:T(8,128)(2,1)} %param.16), kind=kOutput, calls=%fused_computation.44 | convolution fusion | flops 3758096384 | bytes 19791872 | tf_op jit(solution)/shard_map/dot_general | solution.py:39
  101.1 13.9 %convolution_subtract_fusion = f32[256,4096]{1,0:T(8,128)} fusion(f32[256,4096]{1,0:T(8,128)} %fusion.25, bf16[2048,4096]{1,0:T(8,128)(2,1)} %all-gather.6.cloned.1.call-done, bf16[256,2048]{1,0:T(8,128)(2,1)} %gather_fusion, pred[256]{0:T(512)(128)(4,1)S(1)} %compare_and_fusion), kind=kOutput, calls=%fused_computation.10 | convolution fusion | flops 4296540160 | bytes 26214656 | tf_op jit(solution)/shard_map/dot_general | solution.py:53
  115.0 162.8 %all-reduce.2.cloned.1.call-done = f32[256,4096]{1,0:T(8,128)} async-done(((f32[256,4096]{1,0:T(8,128)}), f32[256,4096]{1,0:T(8,128)}) %all-reduce.2.cloned.1.call-update) | async-done | bytes 4194320 | tf_op jit(solution)/shard_map/psum | solution.py:60
  277.8 9.5 %convolution_convert_fusion = bf16[1792,4096]{1,0:T(8,128)(2,1)} fusion(bf16[256,1792]{1,0:T(8,128)(2,1)S(1)} %get-tuple-element.3, f32[256,4096]{1,0:T(8,128)} %all-reduce.2.cloned.1.call-done, bf16[256,4096]{1,0:T(8,128)(2,1)S(1)} %copy-done), kind=kOutput, calls=%fused_computation.1 | convolution fusion | flops 3769630720 | bytes 21889024 | tf_op jit(solution)/shard_map/dot_general | solution.py:75
  287.3 7.5 %constant_dynamic-slice_fusion = bf16[1792,2048]{1,0:T(8,128)(2,1)} fusion(bf16[1792,4096]{1,0:T(8,128)(2,1)} %convolution_convert_fusion, s32[]{:T(128)S(6)} %select_n.26), kind=kLoop, calls=%fused_computation.33 | loop fusion | bytes 14680068 | tf_op jit(solution)/shard_map/dynamic_slice | solution.py:87
  294.9 0.8 collective-permute-start.2
  295.7 11.7 %fusion.17 = f32[256,1792]{1,0:T(8,128)} fusion(bf16[1792,4096]{1,0:T(8,128)(2,1)} %param.16, f32[256,4096]{1,0:T(8,128)} %all-reduce.2.cloned.1.call-done, bf16[256,4096]{1,0:T(8,128)(2,1)S(1)} %copy-done), kind=kOutput, calls=%fused_computation.41 | convolution fusion | flops 3762290688 | bytes 22806528 | tf_op jit(solution)/shard_map/dot_general | solution.py:62
  307.4 10.7 %convolution_convert_fusion.2 = bf16[4096,1792]{1,0:T(8,128)(2,1)} fusion(f32[256,1792]{1,0:T(8,128)} %copy-done.5, f32[256,1792]{1,0:T(8,128)} %fusion.17, f32[256,1792]{1,0:T(8,128)} %get-tuple-element.4, bf16[256,4096]{1,0:T(8,128)(2,1)S(1)} %copy-done, f32[4096]{0:T(1024)S(1)} %bitcast.26, f32[256]{0:T(256)S(1)} %add_rsqrt_fusion.1), kind=kOutput, calls=%fused_computation.3 | convolution fusion | flops 3774218240 | bytes 22299648 | tf_op jit(solution)/shard_map/dot_general | solution.py:69
  318.1 6.6 %constant_dynamic-slice_fusion.2 = bf16[2048,1792]{1,0:T(8,128)(2,1)} fusion(bf16[4096,1792]{1,0:T(8,128)(2,1)} %convolution_convert_fusion.2, s32[]{:T(128)S(6)} %select_n.26), kind=kLoop, calls=%fused_computation.35 | loop fusion | bytes 14680068 | tf_op jit(solution)/shard_map/dynamic_slice | solution.py:85
  324.7 9.8 %convolution_convert_fusion.1 = bf16[4096,1792]{1,0:T(8,128)(2,1)} fusion(f32[256,1792]{1,0:T(8,128)} %fusion.17, f32[256,1792]{1,0:T(8,128)} %copy-done.5, bf16[256,4096]{1,0:T(8,128)(2,1)S(1)} %copy-done, f32[4096]{0:T(1024)S(1)} %bitcast.27, f32[256]{0:T(256)S(1)} %add_rsqrt_fusion.1), kind=kOutput, calls=%fused_computation.2 | convolution fusion | flops 3772383232 | bytes 20464640 | tf_op jit(solution)/shard_map/dot_general | solution.py:72
  334.5 6.6 %constant_dynamic-slice_fusion.1 = bf16[2048,1792]{1,0:T(8,128)(2,1)} fusion(bf16[4096,1792]{1,0:T(8,128)(2,1)} %convolution_convert_fusion.1, s32[]{:T(128)S(6)} %select_n.26), kind=kLoop, calls=%fused_computation.34 | loop fusion | bytes 14680068 | tf_op jit(solution)/shard_map/dynamic_slice | solution.py:86
  341.1 0.5 collective-permute-start.1
  341.6 12.7 %add_convert_fusion = bf16[1792,2048]{1,0:T(8,128)(2,1)} fusion(bf16[1792,2048]{1,0:T(8,128)(2,1)} %collective-permute-done.2, bf16[1792,4096]{1,0:T(8,128)(2,1)} %convolution_convert_fusion, s32[]{:T(128)S(6)} %select_n.25), kind=kLoop, calls=%fused_computation.4 | loop fusion | flops 14680064 | bytes 22020100 | tf_op jit(solution)/shard_map/convert_element_type | solution.py:95
  354.2 10.2 %add_convert_fusion.2 = bf16[2048,1792]{1,0:T(8,128)(2,1)} fusion(bf16[2048,1792]{1,0:T(8,128)(2,1)} %collective-permute-done, bf16[4096,1792]{1,0:T(8,128)(2,1)} %convolution_convert_fusion.2, s32[]{:T(128)S(6)} %select_n.25), kind=kLoop, calls=%fused_computation.6 | loop fusion | flops 14680064 | bytes 22020100 | tf_op jit(solution)/shard_map/convert_element_type | solution.py:93
  364.5 10.1 %add_convert_fusion.1 = bf16[2048,1792]{1,0:T(8,128)(2,1)} fusion(bf16[2048,1792]{1,0:T(8,128)(2,1)} %collective-permute-done.1, bf16[4096,1792]{1,0:T(8,128)(2,1)} %convolution_convert_fusion.1, s32[]{:T(128)S(6)} %select_n.25), kind=kLoop, calls=%fused_computation.5 | loop fusion | flops 14680064 | bytes 22020100 | tf_op jit(solution)/shard_map/convert_element_type | solution.py:94
  (35 shorter events, 0.2 us)
Async XLA Ops:
  7.2 60.2 %all-gather.4.cloned.1.call-start = ((), (), s32[]{:S(2)}) async-start(), calls=%async_computation.1 | async-start | bytes 2359296 | tf_op jit(solution)/shard_map/all_gather | solution.py:26
  7.9 1.2 copy-start.1
  7.9 93.2 %all-gather.6.cloned.1.call-start = ((), (), s32[]{:S(2)}) async-start(), calls=%async_computation.2 | async-start | bytes 25165824 | tf_op jit(solution)/shard_map/all_gather | solution.py:55
  8.7 5.2 %copy-start.3 = (bf16[512]{0:T(512)(128)(2,1)S(1)}, bf16[512]{0:T(512)(128)(2,1)}, u32[]{:S(2)}) copy-start(bf16[512]{0:T(512)(128)(2,1)} %param.13) | copy-start | bytes 3076
  8.7 39.3 %copy-start.2 = (f32[4096]{0:T(1024)S(1)}, f32[4096]{0:T(1024)}, u32[]{:S(2)}) copy-start(f32[4096]{0:T(1024)} %param.10) | copy-start | bytes 49156
  8.7 39.3 %copy-start.4 = (s32[256]{0:T(256)S(1)}, s32[256]{0:T(256)}, u32[]{:S(2)}) copy-start(s32[256]{0:T(256)} %param.17) | copy-start | bytes 3076
  10.2 37.9 %all-to-all-start = ((bf16[128,2,2048]{2,0,1:T(8,128)(2,1)}), bf16[128,2,2048]{2,0,1:T(8,128)(2,1)S(1)}, u32[]{:S(2)}, u32[]{:S(2)}) async-start(bf16[128,2,2048]{2,0,1:T(8,128)(2,1)} %bitcast.22), calls=%async_computation | async-start | bytes 2097152 | tf_op jit(solution)/shard_map/all_to_all | solution.py:41
  13.8 264.1 %all-reduce.2.cloned.1.call-start = ((), (), s32[]{:S(2)}) async-start(), calls=%async_computation.3 | async-start | bytes 8388608 | tf_op jit(solution)/shard_map/psum | solution.py:60
  67.4 14.4 %slice-start = ((s8[14680064]{0:T(1024)(128)(4,1)}), s8[4194304]{0:T(1024)(128)(4,1)S(1)}, s32[]{:S(2)}) async-start(s8[14680064]{0:T(1024)(128)(4,1)} %bitcast.29), calls=%async_computation.4 | async-start | bytes 8388608
  69.6 12.1 %copy-start = (bf16[256,4096]{1,0:T(8,128)(2,1)S(1)}, bf16[256,4096]{1,0:T(8,128)(2,1)}, u32[]{:S(2)}) copy-start(bf16[256,4096]{1,0:T(8,128)(2,1)} %all-gather.4.cloned.1.call-done) | copy-start | bytes 6291460
  69.6 12.5 %slice-start.1 = ((s8[14680064]{0:T(1024)(128)(4,1)}), s8[4194304]{0:T(1024)(128)(4,1)S(1)}, s32[]{:S(2)}) async-start(s8[14680064]{0:T(1024)(128)(4,1)} %bitcast.29), calls=%async_computation.5 | async-start | bytes 8388608
  69.6 14.5 %slice-start.2 = ((s8[14680064]{0:T(1024)(128)(4,1)}), s8[4194304]{0:T(1024)(128)(4,1)S(1)}, s32[]{:S(2)}) async-start(s8[14680064]{0:T(1024)(128)(4,1)} %bitcast.29), calls=%async_computation.6 | async-start | bytes 8388608
  69.6 15.5 %slice-start.3 = ((s8[14680064]{0:T(1024)(128)(4,1)}), s8[2097152]{0:T(1024)(128)(4,1)S(1)}, s32[]{:S(2)}) async-start(s8[14680064]{0:T(1024)(128)(4,1)} %bitcast.29), calls=%async_computation.7 | async-start | bytes 4194304
  85.1 5.3 %copy-start.5 = (f32[256,1792]{1,0:T(8,128)}, f32[256,1792]{1,0:T(8,128)S(1)}, u32[]{:S(2)}) copy-start(f32[256,1792]{1,0:T(8,128)S(1)} %fusion.23) | copy-start | bytes 5505028
  294.9 46.7 %collective-permute-start.2 = (bf16[1792,2048]{1,0:T(8,128)(2,1)}, bf16[1792,2048]{1,0:T(8,128)(2,1)}, u32[]{:S(2)}, u32[]{:S(2)}) collective-permute-start(bf16[1792,2048]{1,0:T(8,128)(2,1)} %constant_dynamic-slice_fusion), channel_id=1, source_target_pairs={{0,1},{1,0},{2,3},{3,2},{4,5},{5,4},{6,7},{7,6},{8,9},{9,8},{10,11... | collective-permute-start | bytes 22020104 | tf_op jit(solution)/shard_map/ppermute | solution.py:10
  324.7 29.5 %collective-permute-start = (bf16[2048,1792]{1,0:T(8,128)(2,1)}, bf16[2048,1792]{1,0:T(8,128)(2,1)}, u32[]{:S(2)}, u32[]{:S(2)}) collective-permute-start(bf16[2048,1792]{1,0:T(8,128)(2,1)} %constant_dynamic-slice_fusion.2), channel_id=1, source_target_pairs={{0,1},{1,0},{2,3},{3,2},{4,5},{5,4},{6,7},{7,6},{8,9},{9,8},{10,11... | collective-permute-start | bytes 22020104 | tf_op jit(solution)/shard_map/ppermute | solution.py:10
  341.1 23.4 %collective-permute-start.1 = (bf16[2048,1792]{1,0:T(8,128)(2,1)}, bf16[2048,1792]{1,0:T(8,128)(2,1)}, u32[]{:S(2)}, u32[]{:S(2)}) collective-permute-start(bf16[2048,1792]{1,0:T(8,128)(2,1)} %constant_dynamic-slice_fusion.1), channel_id=1, source_target_pairs={{0,1},{1,0},{2,3},{3,2},{4,5},{5,4},{6,7},{7,6},{8,9},{9,8},{10,11... | collective-permute-start | bytes 22020104 | tf_op jit(solution)/shard_map/ppermute | solution.py:10
Sparse Core Ops, SparseCore 0:
  10.0 54.8 all-gather.3
  66.4 29.3 all-gather.5
  115.1 162.6 all-reduce.1
where the time goes:
time: 381 us
  waiting for transfers between devices  164 us (43%)
  matrix products  83.6 us (22%)
  blocking collectives  50.5 us (13%)
  other arithmetic  35.8 us (9%)
  local copies, waits for them, and re-layouts  27.9 us (7%)
  between operations  13.9 us (4%)
  starting transfers between devices  5.05 us (1%)
    psum x1, waiting for transfers between devices, on_device(): difference = inputs + lax.psum(output_part, ('tensor', 'section'))  163 us
    all_gather x1, blocking collectives, on_device(): lax.all_gather(student_gain, ('tensor', 'section'), axis=0, tiled=True)  34.1 us
    psum x1, blocking collectives, on_device(): total_sq = lax.psum(local_sq, ('tensor', 'section'))  16.4 us
    dot_general x1, matrix products, on_device(): jnp.dot(arranged, lax.all_gather(proj_weight, 'split', axis=1, tiled=True...  13.9 us
    convert_element_type x1, other arithmetic, on_device(): summed_down.astype(jnp.bfloat16)  12.7 us
    dot_general x1, matrix products, on_device(): gate = jnp.dot(normed, gate_weight, preferred_element_type=jnp.float32)  12.1 us
    dot_general x1, matrix products, on_device(): lax.dot_general(cotangent, down_weight, (((1,), (1,)), ((), ())), preferr...  11.7 us
    dot_general x1, matrix products, on_device(): lax.dot_general(normed, d_gate, contract_rows, preferred_element_type=jnp...  10.7 us
  transfers between devices with their start and end apart: 7, of which 1 were waited for; matrix products, arithmetic and copies ran while one was open for 27% of the time, Pallas kernels for 0%

commit v1 on v0

--- a/solution.py
+++ b/solution.py
@@ -57,7 +57,7 @@
     )
     output_part = output_part - target_part
     total_rows = shard_rows * lax.axis_size("split")
-    difference = inputs + lax.psum(output_part, ("tensor", "section"))
+    difference = inputs + lax.psum(lax.psum(output_part, "section"), "tensor")
     cotangent = (difference * (64.0 / total_rows)).astype(jnp.bfloat16)
     back_hidden = lax.dot_general(
         cotangent, down_weight, (((1,), (1,)), ((), ())), preferred_element_type=jnp.float32

time: 381 us -> 490 us (1.29)
  waiting for transfers between devices: 164 us -> 273 us
    psum x1 -> x2, waiting for transfers between devices: 163 us -> 272 us  [on_device(): difference = inputs + lax.psum(lax.psum(output_part, 'section'), 'tensor')]
  transfers between devices with their start and end apart: 7 -> 8, of which waited for: 1 -> 2; matrix products, arithmetic and copies ran while one was open for 27% -> 21% of each run, Pallas kernels for 0% -> 0%
where the time goes in v1:
time: 490 us
  waiting for transfers between devices  273 us (56%)
  matrix products  83.6 us (17%)
  blocking collectives  50.5 us (10%)
  other arithmetic  35.8 us (7%)
  local copies, waits for them, and re-layouts  27.9 us (6%)
  between operations  14 us (3%)
  starting transfers between devices  5.09 us (1%)
    psum x2, waiting for transfers between devices, on_device(): difference = inputs + lax.psum(lax.psum(output_part, 'section'), 'tensor')  272 us
    all_gather x1, blocking collectives, on_device(): lax.all_gather(student_gain, ('tensor', 'section'), axis=0, tiled=True)  34.1 us
    psum x1, blocking collectives, on_device(): total_sq = lax.psum(local_sq, ('tensor', 'section'))  16.4 us
    dot_general x1, matrix products, on_device(): jnp.dot(arranged, lax.all_gather(proj_weight, 'split', axis=1, tiled=True...  13.9 us
    convert_element_type x1, other arithmetic, on_device(): summed_down.astype(jnp.bfloat16)  12.7 us
    dot_general x1, matrix products, on_device(): gate = jnp.dot(normed, gate_weight, preferred_element_type=jnp.float32)  12.1 us
    dot_general x1, matrix products, on_device(): lax.dot_general(cotangent, down_weight, (((1,), (1,)), ((), ())), preferr...  11.7 us
    dot_general x1, matrix products, on_device(): lax.dot_general(normed, d_gate, contract_rows, preferred_element_type=jnp...  10.7 us
  transfers between devices with their start and end apart: 8, of which 2 were waited for; matrix products, arithmetic and copies ran while one was open for 21% of the time, Pallas kernels for 0%

profile of v1, /device:TPU:1, one launch (start us, length us, event | category | flops | bytes accessed | tf_op | source)
XLA Modules:
  0.0 489.8 jit_solution(424852948299616688)
XLA Ops:
  7.2 0.7 all-gather.4.cloned.1.call-update
  8.0 0.7 all-gather.6.cloned.1.call-update
  8.7 0.4 copy-done.1
  9.1 1.0 copy.17
  10.2 3.6 all-to-all-start
  13.8 34.1 %all-gather = bf16[8,1,512]{2,1,0:T(2,128)(2,1)S(1)} all-gather(bf16[1,1,512]{2,1,0:T(2,128)(2,1)S(1)} %reshape.38), channel_id=1, replica_groups=mesh['groups'=2,'tensor'=4,'section'=2,'split'=2] {'tensor','section'}, dimensions={0}, use_global_device_ids=true | all-gather | bytes 9216 | tf_op jit(solution)/shard_map/all_gather | solution.py:27
  48.1 0.3 multiply_reduce_fusion
  48.4 16.4 %psum.21 = f32[256]{0:T(256)S(1)} all-reduce(f32[256]{0:T(256)S(1)} %bitcast.28), channel_id=1, replica_groups=mesh['groups'=2,'tensor'=4,'section'=2,'split'=2] {'tensor','section'}, use_global_device_ids=true, to_apply=%region_2.3 | all-reduce | flops 256 | bytes 2048 | tf_op jit(solution)/shard_map/psum | solution.py:44
  64.7 0.3 fusion.6
  65.0 2.3 gather_fusion
  67.4 2.2 fusion
  69.7 12.1 %fusion.23 = f32[256,1792]{1,0:T(8,128)S(1)} fusion(bf16[4096,1792]{1,0:T(8,128)(2,1)} %param.14, bf16[256,4096]{1,0:T(8,128)(2,1)} %all-gather.4.cloned.1.call-done, f32[4096]{0:T(1024)S(1)} %bitcast.24, f32[256]{0:T(256)S(1)} %add_rsqrt_fusion.1), kind=kOutput, calls=%fused_computation.43 | convolution fusion | flops 3762290688 | bytes 18629632 | tf_op jit(solution)/shard_map/dot_general | solution.py:35
  81.8 0.3 slice-done.1
  82.1 2.1 slice-done.2
  84.2 0.9 slice-done.3
  85.1 5.3 %multiply_convert_fusion.2 = (bf16[256,1792]{1,0:T(8,128)(2,1)S(1)}, f32[256,1792]{1,0:T(8,128)}) fusion(f32[256,1792]{1,0:T(8,128)S(1)} %fusion.23, bf16[4096,1792]{1,0:T(8,128)(2,1)S(1)} %bitcast.30, bf16[256,4096]{1,0:T(8,128)(2,1)S(1)} %copy-done, f32[4096]{0:T(1024)S(1)} %bitcast.25, f32[256]{0:T(256)S(1)} %add_rsqrt_fusion.1), kind=kOutput, calls=%fused_computation.22 | convolution fusion | flops 3765043200 | bytes 21382144 | tf_op jit(solution)/shard_map/dot_general | solution.py:36
  90.4 10.6 %fusion.25 = f32[256,4096]{1,0:T(8,128)} fusion(bf16[256,1792]{1,0:T(8,128)(2,1)S(1)} %get-tuple-element.3, bf16[1792,4096]{1,0:T(8,128)(2,1)} %param.16), kind=kOutput, calls=%fused_computation.44 | convolution fusion | flops 3758096384 | bytes 19791872 | tf_op jit(solution)/shard_map/dot_general | solution.py:39
  101.1 13.9 %convolution_subtract_fusion = f32[256,4096]{1,0:T(8,128)} fusion(f32[256,4096]{1,0:T(8,128)} %fusion.25, bf16[2048,4096]{1,0:T(8,128)(2,1)} %all-gather.6.cloned.1.call-done, bf16[256,2048]{1,0:T(8,128)(2,1)} %gather_fusion, pred[256]{0:T(512)(128)(4,1)S(1)} %compare_and_fusion), kind=kOutput, calls=%fused_computation.10 | convolution fusion | flops 4296540160 | bytes 26214656 | tf_op jit(solution)/shard_map/dot_general | solution.py:53
  115.0 114.3 %all-reduce.3.cloned.1.call-done = f32[256,4096]{1,0:T(8,128)} async-done(((f32[256,4096]{1,0:T(8,128)}), f32[256,4096]{1,0:T(8,128)}) %all-reduce.3.cloned.1.call-update) | async-done | bytes 4194320 | tf_op jit(solution)/shard_map/psum | solution.py:60
  229.4 157.2 %all-reduce.5.cloned.1.call-done = f32[256,4096]{1,0:T(8,128)} async-done(((f32[256,4096]{1,0:T(8,128)}), f32[256,4096]{1,0:T(8,128)}) %all-reduce.5.cloned.1.call-update) | async-done | bytes 4194320 | tf_op jit(solution)/shard_map/psum | solution.py:60
  386.6 9.5 %convolution_convert_fusion = bf16[1792,4096]{1,0:T(8,128)(2,1)} fusion(bf16[256,1792]{1,0:T(8,128)(2,1)S(1)} %get-tuple-element.3, f32[256,4096]{1,0:T(8,128)} %all-reduce.5.cloned.1.call-done, bf16[256,4096]{1,0:T(8,128)(2,1)S(1)} %copy-done), kind=kOutput, calls=%fused_computation.1 | convolution fusion | flops 3769630720 | bytes 21889024 | tf_op jit(solution)/shard_map/dot_general | solution.py:75
  396.1 7.5 %constant_dynamic-slice_fusion = bf16[1792,2048]{1,0:T(8,128)(2,1)} fusion(bf16[1792,4096]{1,0:T(8,128)(2,1)} %convolution_convert_fusion, s32[]{:T(128)S(6)} %select_n.26), kind=kLoop, calls=%fused_computation.33 | loop fusion | bytes 14680068 | tf_op jit(solution)/shard_map/dynamic_slice | solution.py:87
  403.6 0.8 collective-permute-start.2
  404.5 11.7 %fusion.17 = f32[256,1792]{1,0:T(8,128)} fusion(bf16[1792,4096]{1,0:T(8,128)(2,1)} %param.16, f32[256,4096]{1,0:T(8,128)} %all-reduce.5.cloned.1.call-done, bf16[256,4096]{1,0:T(8,128)(2,1)S(1)} %copy-done), kind=kOutput, calls=%fused_computation.41 | convolution fusion | flops 3762290688 | bytes 22806528 | tf_op jit(solution)/shard_map/dot_general | solution.py:62
  416.2 10.7 %convolution_convert_fusion.2 = bf16[4096,1792]{1,0:T(8,128)(2,1)} fusion(f32[256,1792]{1,0:T(8,128)} %copy-done.5, f32[256,1792]{1,0:T(8,128)} %fusion.17, f32[256,1792]{1,0:T(8,128)} %get-tuple-element.4, bf16[256,4096]{1,0:T(8,128)(2,1)S(1)} %copy-done, f32[4096]{0:T(1024)S(1)} %bitcast.26, f32[256]{0:T(256)S(1)} %add_rsqrt_fusion.1), kind=kOutput, calls=%fused_computation.3 | convolution fusion | flops 3774218240 | bytes 22299648 | tf_op jit(solution)/shard_map/dot_general | solution.py:69
  426.9 6.6 %constant_dynamic-slice_fusion.2 = bf16[2048,1792]{1,0:T(8,128)(2,1)} fusion(bf16[4096,1792]{1,0:T(8,128)(2,1)} %convolution_convert_fusion.2, s32[]{:T(128)S(6)} %select_n.26), kind=kLoop, calls=%fused_computation.35 | loop fusion | bytes 14680068 | tf_op jit(solution)/shard_map/dynamic_slice | solution.py:85
  433.5 9.8 %convolution_convert_fusion.1 = bf16[4096,1792]{1,0:T(8,128)(2,1)} fusion(f32[256,1792]{1,0:T(8,128)} %fusion.17, f32[256,1792]{1,0:T(8,128)} %copy-done.5, bf16[256,4096]{1,0:T(8,128)(2,1)S(1)} %copy-done, f32[4096]{0:T(1024)S(1)} %bitcast.27, f32[256]{0:T(256)S(1)} %add_rsqrt_fusion.1), kind=kOutput, calls=%fused_computation.2 | convolution fusion | flops 3772383232 | bytes 20464640 | tf_op jit(solution)/shard_map/dot_general | solution.py:72
  443.3 6.6 %constant_dynamic-slice_fusion.1 = bf16[2048,1792]{1,0:T(8,128)(2,1)} fusion(bf16[4096,1792]{1,0:T(8,128)(2,1)} %convolution_convert_fusion.1, s32[]{:T(128)S(6)} %select_n.26), kind=kLoop, calls=%fused_computation.34 | loop fusion | bytes 14680068 | tf_op jit(solution)/shard_map/dynamic_slice | solution.py:86
  449.9 0.5 collective-permute-start.1
  450.3 12.7 %add_convert_fusion = bf16[1792,2048]{1,0:T(8,128)(2,1)} fusion(bf16[1792,2048]{1,0:T(8,128)(2,1)} %collective-permute-done.2, bf16[1792,4096]{1,0:T(8,128)(2,1)} %convolution_convert_fusion, s32[]{:T(128)S(6)} %select_n.25), kind=kLoop, calls=%fused_computation.4 | loop fusion | flops 14680064 | bytes 22020100 | tf_op jit(solution)/shard_map/convert_element_type | solution.py:95
  463.0 10.2 %add_convert_fusion.2 = bf16[2048,1792]{1,0:T(8,128)(2,1)} fusion(bf16[2048,1792]{1,0:T(8,128)(2,1)} %collective-permute-done, bf16[4096,1792]{1,0:T(8,128)(2,1)} %convolution_convert_fusion.2, s32[]{:T(128)S(6)} %select_n.25), kind=kLoop, calls=%fused_computation.6 | loop fusion | flops 14680064 | bytes 22020100 | tf_op jit(solution)/shard_map/convert_element_type | solution.py:93
  473.2 10.1 %add_convert_fusion.1 = bf16[2048,1792]{1,0:T(8,128)(2,1)} fusion(bf16[2048,1792]{1,0:T(8,128)(2,1)} %collective-permute-done.1, bf16[4096,1792]{1,0:T(8,128)(2,1)} %convolution_convert_fusion.1, s32[]{:T(128)S(6)} %select_n.25), kind=kLoop, calls=%fused_computation.5 | loop fusion | flops 14680064 | bytes 22020100 | tf_op jit(solution)/shard_map/convert_element_type | solution.py:94
  (38 shorter events, 0.3 us)
Async XLA Ops:
  7.2 60.2 %all-gather.4.cloned.1.call-start = ((), (), s32[]{:S(2)}) async-start(), calls=%async_computation.1 | async-start | bytes 2359296 | tf_op jit(solution)/shard_map/all_gather | solution.py:26
  7.9 1.2 copy-start.1
  7.9 93.2 %all-gather.6.cloned.1.call-start = ((), (), s32[]{:S(2)}) async-start(), calls=%async_computation.2 | async-start | bytes 25165824 | tf_op jit(solution)/shard_map/all_gather | solution.py:55
  8.7 5.2 %copy-start.3 = (bf16[512]{0:T(512)(128)(2,1)S(1)}, bf16[512]{0:T(512)(128)(2,1)}, u32[]{:S(2)}) copy-start(bf16[512]{0:T(512)(128)(2,1)} %param.13) | copy-start | bytes 3076
  8.7 39.3 %copy-start.2 = (f32[4096]{0:T(1024)S(1)}, f32[4096]{0:T(1024)}, u32[]{:S(2)}) copy-start(f32[4096]{0:T(1024)} %param.10) | copy-start | bytes 49156
  8.7 39.3 %copy-start.4 = (s32[256]{0:T(256)S(1)}, s32[256]{0:T(256)}, u32[]{:S(2)}) copy-start(s32[256]{0:T(256)} %param.17) | copy-start | bytes 3076
  10.2 37.9 %all-to-all-start = ((bf16[128,2,2048]{2,0,1:T(8,128)(2,1)}), bf16[128,2,2048]{2,0,1:T(8,128)(2,1)S(1)}, u32[]{:S(2)}, u32[]{:S(2)}) async-start(bf16[128,2,2048]{2,0,1:T(8,128)(2,1)} %bitcast.22), calls=%async_computation | async-start | bytes 2097152 | tf_op jit(solution)/shard_map/all_to_all | solution.py:41
  13.8 215.6 %all-reduce.3.cloned.1.call-start = ((), (), s32[]{:S(2)}) async-start(), calls=%async_computation.3 | async-start | bytes 8388608 | tf_op jit(solution)/shard_map/psum | solution.py:60
  67.4 14.4 %slice-start = ((s8[14680064]{0:T(1024)(128)(4,1)}), s8[4194304]{0:T(1024)(128)(4,1)S(1)}, s32[]{:S(2)}) async-start(s8[14680064]{0:T(1024)(128)(4,1)} %bitcast.29), calls=%async_computation.5 | async-start | bytes 8388608
  69.6 12.1 %copy-start = (bf16[256,4096]{1,0:T(8,128)(2,1)S(1)}, bf16[256,4096]{1,0:T(8,128)(2,1)}, u32[]{:S(2)}) copy-start(bf16[256,4096]{1,0:T(8,128)(2,1)} %all-gather.4.cloned.1.call-done) | copy-start | bytes 6291460
  69.6 12.5 %slice-start.1 = ((s8[14680064]{0:T(1024)(128)(4,1)}), s8[4194304]{0:T(1024)(128)(4,1)S(1)}, s32[]{:S(2)}) async-start(s8[14680064]{0:T(1024)(128)(4,1)} %bitcast.29), calls=%async_computation.6 | async-start | bytes 8388608
  69.6 14.5 %slice-start.2 = ((s8[14680064]{0:T(1024)(128)(4,1)}), s8[4194304]{0:T(1024)(128)(4,1)S(1)}, s32[]{:S(2)}) async-start(s8[14680064]{0:T(1024)(128)(4,1)} %bitcast.29), calls=%async_computation.7 | async-start | bytes 8388608
  69.6 15.5 %slice-start.3 = ((s8[14680064]{0:T(1024)(128)(4,1)}), s8[2097152]{0:T(1024)(128)(4,1)S(1)}, s32[]{:S(2)}) async-start(s8[14680064]{0:T(1024)(128)(4,1)} %bitcast.29), calls=%async_computation.8 | async-start | bytes 4194304
  85.1 5.3 %copy-start.5 = (f32[256,1792]{1,0:T(8,128)}, f32[256,1792]{1,0:T(8,128)S(1)}, u32[]{:S(2)}) copy-start(f32[256,1792]{1,0:T(8,128)S(1)} %fusion.23) | copy-start | bytes 5505028
  115.0 271.6 %all-reduce.5.cloned.1.call-start = ((), (), s32[]{:S(2)}) async-start(), calls=%async_computation.4 | async-start | bytes 8388608 | tf_op jit(solution)/shard_map/psum | solution.py:60
  403.6 46.7 %collective-permute-start.2 = (bf16[1792,2048]{1,0:T(8,128)(2,1)}, bf16[1792,2048]{1,0:T(8,128)(2,1)}, u32[]{:S(2)}, u32[]{:S(2)}) collective-permute-start(bf16[1792,2048]{1,0:T(8,128)(2,1)} %constant_dynamic-slice_fusion), channel_id=1, source_target_pairs={{0,1},{1,0},{2,3},{3,2},{4,5},{5,4},{6,7},{7,6},{8,9},{9,8},{10,11... | collective-permute-start | bytes 22020104 | tf_op jit(solution)/shard_map/ppermute | solution.py:10
  433.5 29.5 %collective-permute-start = (bf16[2048,1792]{1,0:T(8,128)(2,1)}, bf16[2048,1792]{1,0:T(8,128)(2,1)}, u32[]{:S(2)}, u32[]{:S(2)}) collective-permute-start(bf16[2048,1792]{1,0:T(8,128)(2,1)} %constant_dynamic-slice_fusion.2), channel_id=1, source_target_pairs={{0,1},{1,0},{2,3},{3,2},{4,5},{5,4},{6,7},{7,6},{8,9},{9,8},{10,11... | collective-permute-start | bytes 22020104 | tf_op jit(solution)/shard_map/ppermute | solution.py:10
  449.9 23.4 %collective-permute-start.1 = (bf16[2048,1792]{1,0:T(8,128)(2,1)}, bf16[2048,1792]{1,0:T(8,128)(2,1)}, u32[]{:S(2)}, u32[]{:S(2)}) collective-permute-start(bf16[2048,1792]{1,0:T(8,128)(2,1)} %constant_dynamic-slice_fusion.1), channel_id=1, source_target_pairs={{0,1},{1,0},{2,3},{3,2},{4,5},{5,4},{6,7},{7,6},{8,9},{9,8},{10,11... | collective-permute-start | bytes 22020104 | tf_op jit(solution)/shard_map/ppermute | solution.py:10
Sparse Core Ops, SparseCore 0:
  10.0 54.8 all-gather.3
  66.4 29.3 all-gather.5
  115.1 114.2 all-reduce.2
  231.6 154.9 all-reduce.4
